TPU v7x, 32 devices: a whole 2x2x4 slice. The times are simulated.
32 devices in a mesh: section: 4 (over x, core), tensor: 4 (over z), dp: 2 (over y).
Axes of the slice: x: 2, y: 2, z: 4, core: 2. Of those that a mesh axis runs over, the one named last changes fastest.
Arguments:
- layer_in: bfloat16 [2, 2, 4, 2, 128, 2560], P(None, None, 'section', 'dp', 'tensor'), may hold values from -6 to 6
- carry_in: bfloat16 [2, 4, 2, 128, 2560], P(None, 'section', 'dp', 'tensor'), may hold values from -6 to 6
- top_grad: bfloat16 [1, 2, 128, 2560], P(None, 'dp', 'tensor'), may hold values from -6 to 6
- w_qkv: bfloat16 [2, 4, 2560, 2560], P(None, 'section', None, 'tensor'), may hold values from -1 to 1
- w_out: bfloat16 [2, 4, 2048, 2560], P(None, 'section', 'tensor'), may hold values from -0.125 to 0.125
- gain: float32 [2, 4, 2560], P(None, 'section'), may hold values from 0.5 to 1.5
Outputs:
- unit_grads: bfloat16 [2, 2, 4, 2, 128, 2560], P(None, None, 'section', 'dp', 'tensor')
- grad_qkv: bfloat16 [2, 4, 2560, 2560], P(None, 'section', 'dp', 'tensor')
- grad_out: bfloat16 [2, 4, 2048, 2560], P(None, 'section', ('tensor', 'dp'))
- grad_gain: float32 [2, 4, 2560], P(None, 'section')
All inputs are finite; a program needn't handle non-finite values.
Results may differ from a plain program's by a relative error of at most 0.022.
The roundings to bfloat16 on the way count: a program that leaves them out, or rounds other values in their place, can miss the bound.
Values may be sent and summed in bfloat16 or wider, within the bound.
A program may use at most 128 MiB of HBM per device.

v0:
```python
import math
import jax
import jax.numpy as jnp
from jax import lax
from jax.sharding import PartitionSpec as P

KV = 4
HD = 64
GROUP = 8
epsilon = 1e-06
rope_base = 1000000.0


def from_behind(value, axis, steps):
    count = lax.axis_size(axis)
    first, last = (max(0, -steps), min(count, count - steps))
    return lax.ppermute(value, axis, [(source, source + steps) for source in range(first, last)])


def rope_tables(length, head_width):
    half_width = head_width // 2
    exponent = jnp.arange(half_width, dtype=jnp.float32) * (2.0 / head_width)
    frequency = rope_base ** (-exponent)
    angle = jnp.arange(length, dtype=jnp.float32)[:, None] * frequency[None, :]
    return (jnp.cos(angle), jnp.sin(angle))


def rotate(values, cosine_table, sine_table, direction):
    half_width = values.shape[-1] // 2
    table_shape = (values.shape[0],) + (1,) * (values.ndim - 2) + (half_width,)
    cosine = cosine_table.reshape(table_shape)
    sine_part = direction * sine_table.reshape(table_shape)
    lower_half = values[..., :half_width]
    upper_half = values[..., half_width:]
    return jnp.concatenate(
        [
            lower_half * cosine - upper_half * sine_part,
            upper_half * cosine + lower_half * sine_part,
        ],
        axis=-1,
    )


def local(layer_in, carry_in, top_grad, w_qkv, w_out, gain):
    ticks = layer_in.shape[0]
    own_rows = layer_in.shape[4]
    length = own_rows * lax.axis_size("tensor")
    kv_local = KV // lax.axis_size("tensor")
    section_index = lax.axis_index("section")
    at_first = section_index == 0
    at_last = section_index == lax.axis_size("section") - 1
    cosine_table, sine_table = rope_tables(length, HD)
    score_scale = 1.0 / math.sqrt(HD)
    causal_mask = jnp.arange(length)[:, None] >= jnp.arange(length)[None, :]
    layer_rows = layer_in[:, :, 0, 0]
    carried = carry_in[:, 0, 0]
    fresh_grads = top_grad[:, 0]
    weight_qkv = w_qkv[:, 0]
    weight_out = w_out[:, 0]
    gain_rows = gain[:, 0]
    contract_rows = (((0,), (0,)), ((), ()))
    contract_cols = (((1,), (1,)), ((), ()))
    qkv_sums = [
        jnp.zeros(weight_qkv.shape[1:], jnp.float32),
        jnp.zeros(weight_qkv.shape[1:], jnp.float32),
    ]
    out_sums = [
        jnp.zeros(weight_out.shape[1:], jnp.float32),
        jnp.zeros(weight_out.shape[1:], jnp.float32),
    ]
    gain_totals = [
        jnp.zeros(gain_rows.shape[1:], jnp.float32),
        jnp.zeros(gain_rows.shape[1:], jnp.float32),
    ]

    def apply_weights(member, stored):
        normed, grad_full, attended, grad_projected = stored
        qkv_sums[member] = qkv_sums[member] + lax.dot_general(
            normed, grad_projected, contract_rows, preferred_element_type=jnp.float32
        )
        out_sums[member] = out_sums[member] + lax.dot_general(
            attended, grad_full, contract_rows, preferred_element_type=jnp.float32
        )

    inputs = [carried[0], carried[1]]
    per_tick = []
    for position in range(ticks):
        outcome = [None, None]
        pending_members = []
        pending_saved = []
        for member in (1, 0):
            layer_part = layer_rows[position, member]
            grad_output = inputs[member]
            inputs_float = layer_part.astype(jnp.float32)
            inverse = lax.rsqrt(
                jnp.mean(inputs_float * inputs_float, axis=-1, keepdims=True) + epsilon
            )
            unit_rows = inputs_float * inverse
            normed_own = (unit_rows * gain_rows[member]).astype(jnp.bfloat16)
            input_normed = lax.all_gather(normed_own, "tensor", axis=0, tiled=True)
            input_grad_full = lax.all_gather(grad_output, "tensor", axis=0, tiled=True)
            projected = jnp.dot(
                input_normed, weight_qkv[member], preferred_element_type=jnp.float32
            )
            projected = projected.reshape(length, kv_local, GROUP + 2, HD)
            query_rot = rotate(projected[:, :, :GROUP], cosine_table, sine_table, 1.0).astype(
                jnp.bfloat16
            )
            key_rot = rotate(projected[:, :, GROUP], cosine_table, sine_table, 1.0).astype(
                jnp.bfloat16
            )
            value_rows = projected[:, :, GROUP + 1].astype(jnp.bfloat16)
            scores = (
                jnp.einsum("tkgd,ukd->kgtu", query_rot, key_rot, preferred_element_type=jnp.float32)
                * score_scale
            )
            scores = jnp.where(causal_mask, scores, -1e30)
            exponentials = jnp.exp(scores - jnp.max(scores, axis=-1, keepdims=True))
            softmax_rows = exponentials / jnp.sum(exponentials, axis=-1, keepdims=True)
            softmax_low = softmax_rows.astype(jnp.bfloat16)
            input_attended = jnp.einsum(
                "kgtu,ukd->tkgd", softmax_low, value_rows, preferred_element_type=jnp.float32
            )
            input_attended = input_attended.astype(jnp.bfloat16).reshape(
                length, kv_local * GROUP * HD
            )
            grad_attended = lax.dot_general(
                input_grad_full,
                weight_out[member],
                contract_cols,
                preferred_element_type=jnp.float32,
            ).astype(jnp.bfloat16)
            grad_heads = grad_attended.reshape(length, kv_local, GROUP, HD)
            grad_softmax = jnp.einsum(
                "tkgd,ukd->kgtu", grad_heads, value_rows, preferred_element_type=jnp.float32
            )
            row_total = jnp.sum(softmax_rows * grad_softmax, axis=-1, keepdims=True)
            grad_scores = (softmax_rows * (grad_softmax - row_total) * score_scale).astype(
                jnp.bfloat16
            )
            grad_value = jnp.einsum(
                "kgtu,tkgd->ukd", softmax_low, grad_heads, preferred_element_type=jnp.float32
            )
            grad_query = rotate(
                jnp.einsum(
                    "kgtu,ukd->tkgd", grad_scores, key_rot, preferred_element_type=jnp.float32
                ),
                cosine_table,
                sine_table,
                -1.0,
            )
            grad_key = rotate(
                jnp.einsum(
                    "kgtu,tkgd->ukd", grad_scores, query_rot, preferred_element_type=jnp.float32
                ),
                cosine_table,
                sine_table,
                -1.0,
            )
            input_grad_projected = jnp.concatenate(
                [grad_query, grad_key[:, :, None], grad_value[:, :, None]], axis=2
            )
            input_grad_projected = input_grad_projected.reshape(
                length, kv_local * (GROUP + 2) * HD
            ).astype(jnp.bfloat16)
            grad_normed = lax.psum_scatter(
                lax.dot_general(
                    input_grad_projected,
                    weight_qkv[member],
                    contract_cols,
                    preferred_element_type=jnp.float32,
                ).astype(jnp.bfloat16),
                "tensor",
                scatter_dimension=0,
                tiled=True,
            ).astype(jnp.float32)
            grad_unit = grad_normed * gain_rows[member]
            grad_rows = inverse * (
                grad_unit - unit_rows * jnp.mean(grad_unit * unit_rows, axis=-1, keepdims=True)
            )
            grad_input = (grad_output.astype(jnp.float32) + grad_rows).astype(jnp.bfloat16)
            grad_scale = jnp.sum(grad_normed * unit_rows, axis=0)
            grad_input, stored, grad_scale = (
                grad_input,
                (input_normed, input_grad_full, input_attended, input_grad_projected),
                grad_scale,
            )
            outcome[member] = grad_input
            gain_totals[member] = gain_totals[member] + grad_scale
            pending_members.append(member)
            pending_saved.append(stored)
        if position + 1 < ticks:
            upward = from_behind(outcome[1], "section", 1)
            downward = from_behind(outcome[0], "section", -1)
            pending_saved, upward, downward = lax.optimization_barrier(
                (pending_saved, upward, downward)
            )
            inputs = [
                jnp.where(at_last, outcome[1], downward),
                jnp.where(at_first, fresh_grads[position], upward),
            ]
        for member, stored in zip(pending_members, pending_saved):
            apply_weights(member, stored)
        per_tick.append(jnp.stack(outcome))
    grad_qkv_all, grad_out_all = (
        lax.psum_scatter(
            jnp.stack(qkv_sums).astype(jnp.bfloat16), "dp", scatter_dimension=1, tiled=True
        ).astype(jnp.float32),
        lax.psum_scatter(
            jnp.stack(out_sums).astype(jnp.bfloat16), "dp", scatter_dimension=1, tiled=True
        ).astype(jnp.float32),
    )
    gain_total = lax.psum(jnp.stack(gain_totals), ("tensor", "dp"))
    unit_grads = jnp.stack(per_tick)[:, :, None, None]
    return (
        unit_grads,
        grad_qkv_all.astype(jnp.bfloat16)[:, None],
        grad_out_all.astype(jnp.bfloat16)[:, None],
        gain_total[:, None],
    )


def solution(mesh):
    in_specs = (
        P(None, None, "section", "dp", "tensor", None),
        P(None, "section", "dp", "tensor", None),
        P(None, "dp", "tensor", None),
        P(None, "section", None, "tensor"),
        P(None, "section", "tensor", None),
        P(None, "section", None),
    )
    out_specs = (
        P(None, None, "section", "dp", "tensor", None),
        P(None, "section", "dp", "tensor"),
        P(None, "section", ("tensor", "dp"), None),
        P(None, "section", None),
    )
    return jax.shard_map(local, mesh=mesh, in_specs=in_specs, out_specs=out_specs, check_vma=False)
```

profile of v0, /device:TPU:0, one launch (start us, length us, event | category | flops | bytes accessed | tf_op | source)
XLA Modules:
  0.0 479.4 jit_solution(15156333436391977317)
XLA Ops:
  11.8 19.7 %all-gather = bf16[1,1,1,128,2560]{4,3,2,1,0:T(8,128)(2,1)S(1)} all-gather(bf16[1,1,1,32,2560]{4,3,2,1,0:T(8,128)(2,1)S(1)} %get-tuple-element.68), channel_id=2, replica_groups=mesh['section'=4,'tensor'=4,'dp'=2] {'tensor'}, dimensions={3}, use_global_device_ids=true | all-gather | bytes 819200 | tf_op jit(solution)/shard_map/all_gather | solution.py:101
  32.3 2.7 fusion.32
  35.4 17.5 %all_gather.24 = bf16[128,2560]{1,0:T(8,128)(2,1)} all-gather(bf16[32,2560]{1,0:T(8,128)(2,1)S(1)} %get-tuple-element.58), channel_id=1, replica_groups=mesh['section'=4,'tensor'=4,'dp'=2] {'tensor'}, dimensions={0}, use_global_device_ids=true | all-gather | bytes 819200 | tf_op jit(solution)/shard_map/all_gather | solution.py:100
  52.9 16.7 %all_gather.26 = bf16[128,2560]{1,0:T(8,128)(2,1)} all-gather(bf16[32,2560]{1,0:T(8,128)(2,1)S(1)} %get-tuple-element.59), channel_id=1, replica_groups=mesh['section'=4,'tensor'=4,'dp'=2] {'tensor'}, dimensions={0}, use_global_device_ids=true | all-gather | bytes 819200 | tf_op jit(solution)/shard_map/all_gather | solution.py:100
  69.6 6.2 %slice_bitcast_fusion.1 = (bf16[640,2560]{0,1:T(8,128)(2,1)}, bf16[640,2560]{0,1:T(8,128)(2,1)}) fusion(bf16[2,1,2560,640]{3,2,1,0:T(8,128)(2,1)} %param.9), kind=kLoop, calls=%fused_computation.30 | loop fusion | bytes 13107200 | tf_op jit(solution)/shard_map/dot_general | solution.py:102
  75.9 4.0 copy.39
  79.9 2.1 convolution_bitcast_fusion.7
  82.7 5.7 %copy.44 = bf16[640,2560]{1,0:T(8,128)(2,1)} copy(bf16[640,2560]{0,1:T(8,128)(2,1)} %get-tuple-element.51) | data formatting | bytes 6553600 | tf_op jit(solution)/shard_map/dot_general | solution.py:102
  88.4 3.2 convolution_bitcast_fusion.6
  95.4 15.2 %all-gather.1 = bf16[1,1,1,128,2560]{4,3,2,1,0:T(8,128)(2,1)S(1)} all-gather(bf16[1,1,1,32,2560]{4,3,2,1,0:T(8,128)(2,1)S(1)} %copy-done.33), channel_id=3, replica_groups=mesh['section'=4,'tensor'=4,'dp'=2] {'tensor'}, dimensions={3}, use_global_device_ids=true | all-gather | bytes 819200 | tf_op jit(solution)/shard_map/all_gather | solution.py:101
  111.5 3.4 fusion.38
  123.0 4.0 convolution_convert_fusion.2
  129.2 4.0 convolution_convert_fusion.3
  137.2 13.4 %reduce-scatter.9.cloned.1.call-done = bf16[32,2560]{1,0:T(8,128)(2,1)} async-done(((bf16[128,2560]{1,0:T(8,128)(2,1)}), bf16[32,2560]{1,0:T(8,128)(2,1)}) %reduce-scatter.9.cloned.1.call-update) | async-done | bytes 163856 | tf_op jit(solution)/shard_map/reduce_scatter | solution.py:166
  150.5 24.1 %reduce-scatter.7.cloned.1.call-done = bf16[32,2560]{1,0:T(8,128)(2,1)} async-done(((bf16[128,2560]{1,0:T(8,128)(2,1)}), bf16[32,2560]{1,0:T(8,128)(2,1)}) %reduce-scatter.7.cloned.1.call-update) | async-done | bytes 163856 | tf_op jit(solution)/shard_map/reduce_scatter | solution.py:166
  174.7 2.3 fusion.90
  178.8 16.5 %all_gather.30 = bf16[128,2560]{1,0:T(8,128)(2,1)S(1)} all-gather(bf16[32,2560]{1,0:T(8,128)(2,1)S(1)} %get-tuple-element.54), channel_id=1, replica_groups=mesh['section'=4,'tensor'=4,'dp'=2] {'tensor'}, dimensions={0}, use_global_device_ids=true | all-gather | bytes 819200 | tf_op jit(solution)/shard_map/all_gather | solution.py:100
  196.4 15.8 %all_gather.28 = bf16[128,2560]{1,0:T(8,128)(2,1)S(1)} all-gather(bf16[32,2560]{1,0:T(8,128)(2,1)S(1)} %get-tuple-element.55), channel_id=1, replica_groups=mesh['section'=4,'tensor'=4,'dp'=2] {'tensor'}, dimensions={0}, use_global_device_ids=true | all-gather | bytes 819200 | tf_op jit(solution)/shard_map/all_gather | solution.py:100
  214.8 3.0 collective-permute-start
  221.0 17.3 %all_gather.29 = bf16[128,2560]{1,0:T(8,128)(2,1)S(1)} all-gather(bf16[32,2560]{1,0:T(8,128)(2,1)S(1)} %broadcast_select_fusion), channel_id=1, replica_groups=mesh['section'=4,'tensor'=4,'dp'=2] {'tensor'}, dimensions={0}, use_global_device_ids=true | all-gather | bytes 819200 | tf_op jit(solution)/shard_map/all_gather | solution.py:101
  244.0 16.7 %all_gather.31 = bf16[128,2560]{1,0:T(8,128)(2,1)S(1)} all-gather(bf16[32,2560]{1,0:T(8,128)(2,1)S(1)} %bitcast_select_fusion), channel_id=1, replica_groups=mesh['section'=4,'tensor'=4,'dp'=2] {'tensor'}, dimensions={0}, use_global_device_ids=true | all-gather | bytes 819200 | tf_op jit(solution)/shard_map/all_gather | solution.py:101
  261.5 3.5 fusion.41
  272.2 2.0 convolution_convert_fusion
  277.3 4.0 convolution_convert_fusion.1
  281.2 3.2 fusion.189
  284.5 3.4 fusion.3
  289.9 2.7 pad_maximum_fusion.1
  298.0 3.4 pad_maximum_fusion
  302.5 19.2 %reduce-scatter.11.cloned.1.call-done = bf16[32,2560]{1,0:T(8,128)(2,1)} async-done(((bf16[128,2560]{1,0:T(8,128)(2,1)}), bf16[32,2560]{1,0:T(8,128)(2,1)}) %reduce-scatter.11.cloned.1.call-update) | async-done | bytes 163856 | tf_op jit(solution)/shard_map/reduce_scatter | solution.py:166
  323.2 36.0 %psum.7 = f32[2,1,2560]{2,1,0:T(1,128)} all-reduce(f32[2,1,2560]{2,1,0:T(1,128)S(1)} %broadcast_in_dim.33), channel_id=1, replica_groups=mesh['section'=4,'tensor'=4,'dp'=2] {'tensor','dp'}, use_global_device_ids=true, to_apply=%region_30.31 | all-reduce | flops 5120 | bytes 40960 | tf_op jit(solution)/shard_map/psum | solution.py:213
  361.4 28.5 %reduce-scatter.17.cloned.1.call-done = bf16[2,256,2560]{2,1,0:T(8,128)(2,1)} async-done(((bf16[2,512,2560]{2,1,0:T(8,128)(2,1)}), bf16[2,256,2560]{2,1,0:T(8,128)(2,1)}) %reduce-scatter.17.cloned.1.call-update) | async-done | bytes 2621456 | tf_op jit(solution)/shard_map/reduce_scatter | solution.py:209
  389.9 82.6 %reduce-scatter.15.cloned.1.call-done = bf16[2,1280,640]{2,1,0:T(8,128)(2,1)} async-done(((bf16[2,2560,640]{2,1,0:T(8,128)(2,1)}), bf16[2,1280,640]{2,1,0:T(8,128)(2,1)}) %reduce-scatter.15.cloned.1.call-update) | async-done | bytes 3276816 | tf_op jit(solution)/shard_map/reduce_scatter | solution.py:206
  (319 shorter events, 61.7 us)
Async XLA Ops:
  7.2 28.0 %copy-start.1 = (bf16[2,2,1,1,32,2560]{5,4,3,2,1,0:T(8,128)(2,1)S(1)}, bf16[2,2,1,1,32,2560]{5,4,3,2,1,0:T(8,128)(2,1)}, u32[]{:S(2)}) copy-start(bf16[2,2,1,1,32,2560]{5,4,3,2,1,0:T(8,128)(2,1)} %param.6) | copy-start | bytes 1966084
  7.2 143.4 %reduce-scatter.9.cloned.1.call-start = ((), (), s32[]{:S(2)}) async-start(), calls=%async_computation.7 | async-start | bytes 819200 | tf_op jit(solution)/shard_map/reduce_scatter | solution.py:166
  7.2 84.4 %copy-start.88 = (f32[32]{0:T(128)}, f32[32]{0:T(128)S(1)}, u32[]{:S(2)}) copy-start(f32[32]{0:T(128)S(1)} %negate_power_fusion) | copy-start | bytes 388
  7.3 85.9 %copy-start.49 = (pred[128,128]{0,1:T(8,128)(4,1)}, pred[128,128]{0,1:T(8,128)(4,1)S(1)}, u32[]{:S(2)}) copy-start(pred[128,128]{0,1:T(8,128)(4,1)S(1)} %iota_compare_fusion) | copy-start | bytes 49156
  9.3 26.1 %copy-start.42 = (f32[2560]{0:T(1024)}, f32[2560]{0:T(1024)S(1)}, u32[]{:S(2)}) copy-start(f32[2560]{0:T(1024)S(1)} %get-tuple-element.49) | copy-start | bytes 30724
  10.1 82.3 %copy-start.45 = (f32[128,32]{0,1:T(8,128)}, f32[128,32]{0,1:T(8,128)S(1)}, u32[]{:S(2)}) copy-start(f32[128,32]{0,1:T(8,128)S(1)} %get-tuple-element.112) | copy-start | bytes 49156
  10.1 82.3 %copy-start.59 = (f32[128,32]{0,1:T(8,128)}, f32[128,32]{0,1:T(8,128)S(1)}, u32[]{:S(2)}) copy-start(f32[128,32]{0,1:T(8,128)S(1)} %get-tuple-element.111) | copy-start | bytes 49156
  35.1 58.4 %copy-start.63 = (bf16[128,512]{0,1:T(8,128)(2,1)}, bf16[128,512]{0,1:T(8,128)(2,1)S(1)}, u32[]{:S(2)}) copy-start(bf16[128,512]{0,1:T(8,128)(2,1)S(1)} %copy.40) | copy-start | bytes 393220
  35.2 40.7 %copy-start.92 = (f32[32]{0:T(128)}, f32[32]{0:T(128)S(1)}, u32[]{:S(2)}) copy-start(f32[32]{0:T(128)S(1)} %get-tuple-element.129) | copy-start | bytes 388
  35.2 40.7 %copy-start.94 = (f32[32]{0:T(128)}, f32[32]{0:T(128)S(1)}, u32[]{:S(2)}) copy-start(f32[32]{0:T(128)S(1)} %get-tuple-element.130) | copy-start | bytes 388
  127.0 47.6 %reduce-scatter.7.cloned.1.call-start = ((), (), s32[]{:S(2)}) async-start(), calls=%async_computation.6 | async-start | bytes 819200 | tf_op jit(solution)/shard_map/reduce_scatter | solution.py:166
  133.1 41.5 %copy-start.43 = (f32[2560]{0:T(1024)S(1)}, f32[2560]{0:T(1024)}, u32[]{:S(2)}) copy-start(f32[2560]{0:T(1024)} %copy-done.42) | copy-start | bytes 30724
  133.2 41.5 %copy-start.93 = (f32[32]{0:T(128)S(1)}, f32[32]{0:T(128)}, u32[]{:S(2)}) copy-start(f32[32]{0:T(128)} %copy-done.92) | copy-start | bytes 388
  133.2 41.5 %copy-start.95 = (f32[32]{0:T(128)S(1)}, f32[32]{0:T(128)}, u32[]{:S(2)}) copy-start(f32[32]{0:T(128)} %copy-done.94) | copy-start | bytes 388
  133.2 169.3 %reduce-scatter.13.cloned.1.call-start = ((), (), s32[]{:S(2)}) async-start(), calls=%async_computation.9 | async-start | bytes 819200 | tf_op jit(solution)/shard_map/reduce_scatter | solution.py:166
  174.7 20.7 %copy-start = (bf16[640,2560]{1,0:T(8,128)(2,1)S(1)}, bf16[640,2560]{1,0:T(8,128)(2,1)}, u32[]{:S(2)}) copy-start(bf16[640,2560]{1,0:T(8,128)(2,1)} %copy.44) | copy-start | bytes 9830404
  178.8 34.6 %copy-start.31 = (bf16[32,2560]{1,0:T(8,128)(2,1)}, bf16[32,2560]{1,0:T(8,128)(2,1)S(1)}, u32[]{:S(2)}) copy-start(bf16[32,2560]{1,0:T(8,128)(2,1)S(1)} %get-tuple-element.52) | copy-start | bytes 491524
  178.8 41.5 %copy-start.19 = (bf16[32,2560]{1,0:T(8,128)(2,1)}, bf16[32,2560]{1,0:T(8,128)(2,1)S(1)}, u32[]{:S(2)}) copy-start(bf16[32,2560]{1,0:T(8,128)(2,1)S(1)} %get-tuple-element.53) | copy-start | bytes 491524
  195.3 43.9 %slice-start.2 = ((s8[5242880]{0:T(1024)(128)(4,1)}), s8[1048576]{0:T(1024)(128)(4,1)S(1)}, s32[]{:S(2)}) async-start(s8[5242880]{0:T(1024)(128)(4,1)} %bitcast.493), calls=%async_computation.14 | async-start | bytes 2097152
  196.4 21.4 %copy-start.90 = (f32[32]{0:T(128)S(1)}, f32[32]{0:T(128)}, u32[]{:S(2)}) copy-start(f32[32]{0:T(128)} %copy-done.88) | copy-start | bytes 388
  196.4 21.6 %copy-start.50 = (pred[128,128]{0,1:T(8,128)(4,1)S(1)}, pred[128,128]{0,1:T(8,128)(4,1)}, u32[]{:S(2)}) copy-start(pred[128,128]{0,1:T(8,128)(4,1)} %copy-done.49) | copy-start | bytes 49156
  212.2 27.1 %slice-start.3 = ((s8[5242880]{0:T(1024)(128)(4,1)}), s8[4194304]{0:T(1024)(128)(4,1)S(1)}, s32[]{:S(2)}) async-start(s8[5242880]{0:T(1024)(128)(4,1)} %bitcast.493), calls=%async_computation.15 | async-start | bytes 8388608
  213.4 6.9 %collective-permute-start.1 = (bf16[32,2560]{1,0:T(8,128)(2,1)S(1)}, bf16[32,2560]{1,0:T(8,128)(2,1)S(1)}, u32[]{:S(2)}, u32[]{:S(2)}) collective-permute-start(bf16[32,2560]{1,0:T(8,128)(2,1)S(1)} %get-tuple-element.52), channel_id=1, source_target_pairs={{8,0},{16,8},{24,16},{9,1},{17,9},{25,17},{10,2},{18,10},{26,18},{... | collective-permute-start | bytes 491528 | tf_op jit(solution)/shard_map/ppermute | solution.py:17
  214.8 5.5 %collective-permute-start = (bf16[32,2560]{1,0:T(8,128)(2,1)S(1)}, bf16[32,2560]{1,0:T(8,128)(2,1)S(1)}, u32[]{:S(2)}, u32[]{:S(2)}) collective-permute-start(bf16[32,2560]{1,0:T(8,128)(2,1)S(1)} %get-tuple-element.53), channel_id=1, source_target_pairs={{0,8},{8,16},{16,24},{1,9},{9,17},{17,25},{2,10},{10,18},{18,26},{... | collective-permute-start | bytes 491528 | tf_op jit(solution)/shard_map/ppermute | solution.py:17
  218.4 23.0 %copy-start.84 = (f32[8,128]{1,0:T(8,128)}, f32[8,128]{1,0:T(8,128)S(1)}, u32[]{:S(2)}) copy-start(f32[8,128]{1,0:T(8,128)S(1)} %fusion.53) | copy-start | bytes 12292
  274.2 47.5 %reduce-scatter.11.cloned.1.call-start = ((), (), s32[]{:S(2)}) async-start(), calls=%async_computation.8 | async-start | bytes 819200 | tf_op jit(solution)/shard_map/reduce_scatter | solution.py:166
  284.4 105.5 %reduce-scatter.17.cloned.1.call-start = ((), (), s32[]{:S(2)}) async-start(), calls=%async_computation.11 | async-start | bytes 7864320 | tf_op jit(solution)/shard_map/reduce_scatter | solution.py:209
  292.6 179.9 %reduce-scatter.15.cloned.1.call-start = ((), (), s32[]{:S(2)}) async-start(), calls=%async_computation.10 | async-start | bytes 9830400 | tf_op jit(solution)/shard_map/reduce_scatter | solution.py:206
  301.4 21.6 %copy-start.75 = (f32[2560]{0:T(1024)S(1)}, f32[2560]{0:T(1024)}, u32[]{:S(2)}) copy-start(f32[2560]{0:T(1024)} %get-tuple-element.43) | copy-start | bytes 30724
  301.4 21.7 %copy-start.74 = (f32[2560]{0:T(1024)S(1)}, f32[2560]{0:T(1024)}, u32[]{:S(2)}) copy-start(f32[2560]{0:T(1024)} %get-tuple-element.34) | copy-start | bytes 30724
  301.5 57.7 %copy-start.22 = (bf16[32,2560]{1,0:T(8,128)(2,1)S(1)}, bf16[32,2560]{1,0:T(8,128)(2,1)}, u32[]{:S(2)}) copy-start(bf16[32,2560]{1,0:T(8,128)(2,1)} %copy-done.21) | copy-start | bytes 491524
  301.5 57.7 %copy-start.24 = (bf16[32,2560]{1,0:T(8,128)(2,1)S(1)}, bf16[32,2560]{1,0:T(8,128)(2,1)}, u32[]{:S(2)}) copy-start(bf16[32,2560]{1,0:T(8,128)(2,1)} %copy-done.23) | copy-start | bytes 491524
  (80 other events, 446.7 us)
Sparse Core Ops, SparseCore 0:
  127.1 23.3 reduce-scatter.8
  153.4 21.2 reduce-scatter.6
  274.4 23.2 reduce-scatter.12
  300.4 21.2 reduce-scatter.10
  324.4 65.4 reduce-scatter.16
  392.6 79.8 reduce-scatter.14
where the time goes:
time: 481 us; the launch traced here: 479 us
  blocking collectives  171 us (36%)
  waiting for transfers between devices  168 us (35%)
  matrix products  64 us (13%)
  local copies, waits for them, and re-layouts  32.3 us (7%)
  other arithmetic  23 us (5%)
  between operations  15.6 us (3%)
  starting transfers between devices  4.93 us (1%)
    reduce_scatter x1, waiting for transfers between devices, local(): lax.psum_scatter(jnp.stack(qkv_sums).astype(jnp.bfloat16), 'dp', scatter_...  82.6 us
    all_gather x4, blocking collectives, local(): input_grad_full = lax.all_gather(grad_output, 'tensor', axis=0, tiled=True)  68.9 us
    all_gather x4, blocking collectives, local(): input_normed = lax.all_gather(normed_own, 'tensor', axis=0, tiled=True)  66.6 us
    reduce_scatter x4, waiting for transfers between devices, local(): lax.psum_scatter(lax.dot_general(input_grad_projected, weight_qkv[member]...  56.8 us
    psum x1, blocking collectives, local(): gain_total = lax.psum(jnp.stack(gain_totals), ('tensor', 'dp'))  36 us
    reduce_scatter x1, waiting for transfers between devices, local(): lax.psum_scatter(jnp.stack(out_sums).astype(jnp.bfloat16), 'dp', scatter_...  28.5 us
    dot_general x3, local copies, waits for them, and re-layouts, local(): jnp.dot(input_normed, weight_qkv[member], preferred_element_type=jnp.floa...  15.9 us
    dot_general x4, matrix products, local(): lax.dot_general(input_grad_projected, weight_qkv[member], contract_cols,...  14 us
  transfers between devices with their start and end apart: 8, of which 5 were waited for; matrix products, arithmetic and copies ran while one was open for 8% of the time, Pallas kernels for 0%

commit v1 on v0

--- a/solution.py
+++ b/solution.py
@@ -97,7 +97,10 @@
             )
             unit_rows = inputs_float * inverse
             normed_own = (unit_rows * gain_rows[member]).astype(jnp.bfloat16)
-            input_normed = lax.all_gather(normed_own, "tensor", axis=0, tiled=True)
+            input_normed = jnp.concatenate(
+                lax.all_to_all(jnp.stack([normed_own] * lax.axis_size("tensor")), "tensor", 0, 0),
+                axis=0,
+            )
             input_grad_full = lax.all_gather(grad_output, "tensor", axis=0, tiled=True)
             projected = jnp.dot(
                 input_normed, weight_qkv[member], preferred_element_type=jnp.float32

time: 481 us -> 464 us (0.965)
  blocking collectives: 171 us -> 136 us
  starting transfers between devices: 4.93 us -> 25.6 us
    all_gather x4 -> x0, blocking collectives: 66.6 us -> none  [local(): input_normed = lax.all_gather(normed_own, 'tensor', axis=0, tiled=True)]
    all_gather x4, blocking collectives: 68.9 us -> 100 us  [local(): input_grad_full = lax.all_gather(grad_output, 'tensor', axis=0, tiled=True)]
    all_to_all x0 -> x4, starting transfers between devices: none -> 20.2 us  [local(): lax.all_to_all(jnp.stack([normed_own] * lax.axis_size('tensor')), 'tensor...]
    unnamed x208 -> x110, local copies, waits for them, and re-layouts: 10.3 us -> 7 us
  transfers between devices with their start and end apart: 8 -> 12, of which waited for: 5 -> 5; matrix products, arithmetic and copies ran while one was open for 8% -> 18% of each run, Pallas kernels for 0% -> 0%
where the time goes in v1:
time: 464 us; the launch traced here: 463 us
  waiting for transfers between devices  167 us (36%)
  blocking collectives  136 us (29%)
  matrix products  62.4 us (13%)
  local copies, waits for them, and re-layouts  33.9 us (7%)
  starting transfers between devices  25.6 us (6%)
  other arithmetic  22 us (5%)
  between operations  15.2 us (3%)
    all_gather x4, blocking collectives, local(): input_grad_full = lax.all_gather(grad_output, 'tensor', axis=0, tiled=True)  100 us
    reduce_scatter x1, waiting for transfers between devices, local(): lax.psum_scatter(jnp.stack(qkv_sums).astype(jnp.bfloat16), 'dp', scatter_...  82.6 us
    reduce_scatter x4, waiting for transfers between devices, local(): lax.psum_scatter(lax.dot_general(input_grad_projected, weight_qkv[member]...  56.1 us
    psum x1, blocking collectives, local(): gain_total = lax.psum(jnp.stack(gain_totals), ('tensor', 'dp'))  36.1 us
    reduce_scatter x1, waiting for transfers between devices, local(): lax.psum_scatter(jnp.stack(out_sums).astype(jnp.bfloat16), 'dp', scatter_...  28.5 us
    all_to_all x4, starting transfers between devices, local(): lax.all_to_all(jnp.stack([normed_own] * lax.axis_size('tensor')), 'tensor...  20.2 us
    dot_general x3, local copies, waits for them, and re-layouts, local(): jnp.dot(input_normed, weight_qkv[member], preferred_element_type=jnp.floa...  16.2 us
    dot_general x4, matrix products, local(): lax.dot_general(input_grad_full, weight_out[member], contract_cols, prefe...  12.3 us
  transfers between devices with their start and end apart: 12, of which 5 were waited for; matrix products, arithmetic and copies ran while one was open for 18% of the time, Pallas kernels for 0%

profile of v1, /device:TPU:0, one launch (start us, length us, event | category | flops | bytes accessed | tf_op | source)
XLA Modules:
  0.0 462.5 jit_solution(14137303537779229546)
XLA Ops:
  11.3 6.3 %all-to-all-start = ((bf16[4,32,2560]{2,1,0:T(8,128)(2,1)}), bf16[4,32,2560]{2,1,0:T(8,128)(2,1)S(1)}, u32[]{:S(2)}, u32[]{:S(2)}) async-start(bf16[4,32,2560]{2,1,0:T(8,128)(2,1)} %stack.84), calls=%async_computation | async-start | bytes 1310720 | tf_op jit(solution)/shard_map/all_to_all | solution.py:101
  17.6 28.7 %all-gather = bf16[1,1,1,128,2560]{4,3,2,1,0:T(8,128)(2,1)S(1)} all-gather(bf16[1,1,1,32,2560]{4,3,2,1,0:T(8,128)(2,1)S(1)} %get-tuple-element.68), channel_id=2, replica_groups=mesh['section'=4,'tensor'=4,'dp'=2] {'tensor'}, dimensions={3}, use_global_device_ids=true | all-gather | bytes 819200 | tf_op jit(solution)/shard_map/all_gather | solution.py:104
  46.3 2.9 fusion.32
  49.3 16.6 %all-gather.1 = bf16[1,1,1,128,2560]{4,3,2,1,0:T(8,128)(2,1)S(1)} all-gather(bf16[1,1,1,32,2560]{4,3,2,1,0:T(8,128)(2,1)S(1)} %get-tuple-element.69), channel_id=3, replica_groups=mesh['section'=4,'tensor'=4,'dp'=2] {'tensor'}, dimensions={3}, use_global_device_ids=true | all-gather | bytes 819200 | tf_op jit(solution)/shard_map/all_gather | solution.py:104
  65.9 6.5 %slice_bitcast_fusion.1 = (bf16[640,2560]{0,1:T(8,128)(2,1)}, bf16[640,2560]{0,1:T(8,128)(2,1)}) fusion(bf16[2,1,2560,640]{3,2,1,0:T(8,128)(2,1)} %param.9), kind=kLoop, calls=%fused_computation.30 | loop fusion | bytes 13107200 | tf_op jit(solution)/shard_map/dot_general | solution.py:105
  73.3 4.9 %all-to-all-start.1 = ((bf16[4,32,2560]{2,1,0:T(8,128)(2,1)}), bf16[4,32,2560]{2,1,0:T(8,128)(2,1)}, u32[]{:S(2)}, u32[]{:S(2)}) async-start(bf16[4,32,2560]{2,1,0:T(8,128)(2,1)} %stack.86), calls=%async_computation.2 | async-start | bytes 1310720 | tf_op jit(solution)/shard_map/all_to_all | solution.py:101
  78.2 2.7 fusion.38
  82.4 4.0 copy.39
  86.4 5.7 %copy.44 = bf16[640,2560]{1,0:T(8,128)(2,1)} copy(bf16[640,2560]{0,1:T(8,128)(2,1)} %get-tuple-element.51) | data formatting | bytes 6553600 | tf_op jit(solution)/shard_map/dot_general | solution.py:105
  95.1 3.2 convolution_bitcast_fusion.6
  106.7 4.0 convolution_convert_fusion.3
  112.6 16.2 %reduce-scatter.9.cloned.1.call-done = bf16[32,2560]{1,0:T(8,128)(2,1)} async-done(((bf16[128,2560]{1,0:T(8,128)(2,1)}), bf16[32,2560]{1,0:T(8,128)(2,1)}) %reduce-scatter.9.cloned.1.call-update) | async-done | bytes 163856 | tf_op jit(solution)/shard_map/reduce_scatter | solution.py:169
  128.8 24.1 %reduce-scatter.7.cloned.1.call-done = bf16[32,2560]{1,0:T(8,128)(2,1)} async-done(((bf16[128,2560]{1,0:T(8,128)(2,1)}), bf16[32,2560]{1,0:T(8,128)(2,1)}) %reduce-scatter.7.cloned.1.call-update) | async-done | bytes 163856 | tf_op jit(solution)/shard_map/reduce_scatter | solution.py:169
  154.7 2.4 fusion.87
  158.4 3.7 collective-permute-start
  164.9 4.2 all-to-all-start.3
  170.7 27.6 %all_gather.15 = bf16[128,2560]{1,0:T(8,128)(2,1)S(1)} all-gather(bf16[32,2560]{1,0:T(8,128)(2,1)S(1)} %bitcast_select_fusion), channel_id=1, replica_groups=mesh['section'=4,'tensor'=4,'dp'=2] {'tensor'}, dimensions={0}, use_global_device_ids=true | all-gather | bytes 819200 | tf_op jit(solution)/shard_map/all_gather | solution.py:104
  199.2 3.3 fusion.41
  207.6 4.8 %all-to-all-start.2 = ((bf16[4,32,2560]{2,1,0:T(8,128)(2,1)}), bf16[4,32,2560]{2,1,0:T(8,128)(2,1)}, u32[]{:S(2)}, u32[]{:S(2)}) async-start(bf16[4,32,2560]{2,1,0:T(8,128)(2,1)} %stack.90), calls=%async_computation.4 | async-start | bytes 1310720 | tf_op jit(solution)/shard_map/all_to_all | solution.py:101
  212.4 27.1 %all_gather.14 = bf16[128,2560]{1,0:T(8,128)(2,1)S(1)} all-gather(bf16[32,2560]{1,0:T(8,128)(2,1)} %broadcast_select_fusion), channel_id=1, replica_groups=mesh['section'=4,'tensor'=4,'dp'=2] {'tensor'}, dimensions={0}, use_global_device_ids=true | all-gather | bytes 819200 | tf_op jit(solution)/shard_map/all_gather | solution.py:104
  240.4 3.3 fusion.35
  245.4 3.1 convolution_bitcast_fusion.4
  259.4 4.0 convolution_convert_fusion.1
  263.4 3.1 fusion.189
  266.6 3.6 fusion.3
  273.2 2.8 pad_maximum_fusion.1
  277.0 2.2 fusion.186
  284.6 3.4 pad_maximum_fusion
  289.1 15.8 %reduce-scatter.11.cloned.1.call-done = bf16[32,2560]{1,0:T(8,128)(2,1)} async-done(((bf16[128,2560]{1,0:T(8,128)(2,1)}), bf16[32,2560]{1,0:T(8,128)(2,1)}) %reduce-scatter.11.cloned.1.call-update) | async-done | bytes 163856 | tf_op jit(solution)/shard_map/reduce_scatter | solution.py:169
  306.4 36.1 %psum.7 = f32[2,1,2560]{2,1,0:T(1,128)} all-reduce(f32[2,1,2560]{2,1,0:T(1,128)S(1)} %broadcast_in_dim.33), channel_id=1, replica_groups=mesh['section'=4,'tensor'=4,'dp'=2] {'tensor','dp'}, use_global_device_ids=true, to_apply=%region_30.31 | all-reduce | flops 5120 | bytes 40960 | tf_op jit(solution)/shard_map/psum | solution.py:216
  344.6 28.5 %reduce-scatter.17.cloned.1.call-done = bf16[2,256,2560]{2,1,0:T(8,128)(2,1)} async-done(((bf16[2,512,2560]{2,1,0:T(8,128)(2,1)}), bf16[2,256,2560]{2,1,0:T(8,128)(2,1)}) %reduce-scatter.17.cloned.1.call-update) | async-done | bytes 2621456 | tf_op jit(solution)/shard_map/reduce_scatter | solution.py:212
  373.1 82.6 %reduce-scatter.15.cloned.1.call-done = bf16[2,1280,640]{2,1,0:T(8,128)(2,1)} async-done(((bf16[2,2560,640]{2,1,0:T(8,128)(2,1)}), bf16[2,1280,640]{2,1,0:T(8,128)(2,1)}) %reduce-scatter.15.cloned.1.call-update) | async-done | bytes 3276816 | tf_op jit(solution)/shard_map/reduce_scatter | solution.py:209
  (229 shorter events, 59.9 us)
Async XLA Ops:
  7.2 10.4 %copy-start.15 = (bf16[2,1,1,32,2560]{4,3,2,1,0:T(8,128)(2,1)S(1)}, bf16[2,1,1,32,2560]{4,3,2,1,0:T(8,128)(2,1)}, u32[]{:S(2)}) copy-start(bf16[2,1,1,32,2560]{4,3,2,1,0:T(8,128)(2,1)} %param.7) | copy-start | bytes 983044
  11.3 61.1 %all-to-all-start = ((bf16[4,32,2560]{2,1,0:T(8,128)(2,1)}), bf16[4,32,2560]{2,1,0:T(8,128)(2,1)S(1)}, u32[]{:S(2)}, u32[]{:S(2)}) async-start(bf16[4,32,2560]{2,1,0:T(8,128)(2,1)} %stack.84), calls=%async_computation | async-start | bytes 1310720 | tf_op jit(solution)/shard_map/all_to_all | solution.py:101
  46.3 26.0 %copy-start.5 = (bf16[1,1,1,128,2560]{4,3,2,1,0:T(8,128)(2,1)}, bf16[1,1,1,128,2560]{4,3,2,1,0:T(8,128)(2,1)S(1)}, u32[]{:S(2)}) copy-start(bf16[1,1,1,128,2560]{4,3,2,1,0:T(8,128)(2,1)S(1)} %all-gather) | copy-start | bytes 1966084
  65.9 12.3 %copy-start.7 = (bf16[1,1,1,128,2560]{4,3,2,1,0:T(8,128)(2,1)}, bf16[1,1,1,128,2560]{4,3,2,1,0:T(8,128)(2,1)S(1)}, u32[]{:S(2)}) copy-start(bf16[1,1,1,128,2560]{4,3,2,1,0:T(8,128)(2,1)S(1)} %all-gather.1) | copy-start | bytes 1966084
  72.4 10.0 %copy-start.1 = (bf16[4,32,2560]{2,1,0:T(8,128)(2,1)}, bf16[4,32,2560]{2,1,0:T(8,128)(2,1)S(1)}, u32[]{:S(2)}) copy-start(bf16[4,32,2560]{2,1,0:T(8,128)(2,1)S(1)} %all-to-all-done) | copy-start | bytes 1966084
  73.3 21.8 %all-to-all-start.1 = ((bf16[4,32,2560]{2,1,0:T(8,128)(2,1)}), bf16[4,32,2560]{2,1,0:T(8,128)(2,1)}, u32[]{:S(2)}, u32[]{:S(2)}) async-start(bf16[4,32,2560]{2,1,0:T(8,128)(2,1)} %stack.86), calls=%async_computation.2 | async-start | bytes 1310720 | tf_op jit(solution)/shard_map/all_to_all | solution.py:101
  78.2 50.6 %reduce-scatter.9.cloned.1.call-start = ((), (), s32[]{:S(2)}) async-start(), calls=%async_computation.11 | async-start | bytes 819200 | tf_op jit(solution)/shard_map/reduce_scatter | solution.py:169
  92.1 9.2 %copy-start.41 = (f32[32]{0:T(128)}, f32[32]{0:T(128)S(1)}, u32[]{:S(2)}) copy-start(f32[32]{0:T(128)S(1)} %negate_power_fusion) | copy-start | bytes 388
  95.1 3.8 copy-start.32
  104.5 48.4 %reduce-scatter.7.cloned.1.call-start = ((), (), s32[]{:S(2)}) async-start(), calls=%async_computation.10 | async-start | bytes 819200 | tf_op jit(solution)/shard_map/reduce_scatter | solution.py:169
  106.7 46.3 %copy-start.44 = (f32[32]{0:T(128)S(1)}, f32[32]{0:T(128)}, u32[]{:S(2)}) copy-start(f32[32]{0:T(128)} %copy-done.43) | copy-start | bytes 388
  106.7 46.3 %copy-start.46 = (f32[32]{0:T(128)S(1)}, f32[32]{0:T(128)}, u32[]{:S(2)}) copy-start(f32[32]{0:T(128)} %copy-done.45) | copy-start | bytes 388
  154.6 3.7 copy-start.47
  154.7 3.7 copy-start.49
  157.1 12.0 %collective-permute-start.1 = (bf16[32,2560]{1,0:T(8,128)(2,1)}, bf16[32,2560]{1,0:T(8,128)(2,1)}, u32[]{:S(2)}, u32[]{:S(2)}) collective-permute-start(bf16[32,2560]{1,0:T(8,128)(2,1)} %get-tuple-element.52), channel_id=1, source_target_pairs={{8,0},{16,8},{24,16},{9,1},{17,9},{25,17},{10,2},{18,10},{26,18},{... | collective-permute-start | bytes 491528 | tf_op jit(solution)/shard_map/ppermute | solution.py:17
  158.4 10.7 %collective-permute-start = (bf16[32,2560]{1,0:T(8,128)(2,1)S(1)}, bf16[32,2560]{1,0:T(8,128)(2,1)}, u32[]{:S(2)}, u32[]{:S(2)}) collective-permute-start(bf16[32,2560]{1,0:T(8,128)(2,1)S(1)} %get-tuple-element.53), channel_id=1, source_target_pairs={{0,8},{8,16},{16,24},{1,9},{9,17},{17,25},{2,10},{10,18},{18,26},{... | collective-permute-start | bytes 491528 | tf_op jit(solution)/shard_map/ppermute | solution.py:17
  164.9 40.9 %all-to-all-start.3 = ((bf16[4,32,2560]{2,1,0:T(8,128)(2,1)}), bf16[4,32,2560]{2,1,0:T(8,128)(2,1)}, u32[]{:S(2)}, u32[]{:S(2)}) async-start(bf16[4,32,2560]{2,1,0:T(8,128)(2,1)} %stack.92), calls=%async_computation.6 | async-start | bytes 1310720 | tf_op jit(solution)/shard_map/all_to_all | solution.py:101
  207.6 42.3 %all-to-all-start.2 = ((bf16[4,32,2560]{2,1,0:T(8,128)(2,1)}), bf16[4,32,2560]{2,1,0:T(8,128)(2,1)}, u32[]{:S(2)}, u32[]{:S(2)}) async-start(bf16[4,32,2560]{2,1,0:T(8,128)(2,1)} %stack.90), calls=%async_computation.4 | async-start | bytes 1310720 | tf_op jit(solution)/shard_map/all_to_all | solution.py:101
  212.4 76.6 %reduce-scatter.13.cloned.1.call-start = ((), (), s32[]{:S(2)}) async-start(), calls=%async_computation.13 | async-start | bytes 819200 | tf_op jit(solution)/shard_map/reduce_scatter | solution.py:169
  252.7 5.3 %copy-start.39 = (f32[8,128]{1,0:T(8,128)}, f32[8,128]{1,0:T(8,128)S(1)}, u32[]{:S(2)}) copy-start(f32[8,128]{1,0:T(8,128)S(1)} %fusion.53) | copy-start | bytes 12292
  258.0 46.9 %reduce-scatter.11.cloned.1.call-start = ((), (), s32[]{:S(2)}) async-start(), calls=%async_computation.12 | async-start | bytes 819200 | tf_op jit(solution)/shard_map/reduce_scatter | solution.py:169
  258.3 5.1 %copy-start.24 = (bf16[128,1,10,64]{0,3,2,1:T(8,128)(2,1)}, bf16[128,1,10,64]{0,3,2,1:T(8,128)(2,1)S(1)}, u32[]{:S(2)}) copy-start(bf16[128,1,10,64]{0,3,2,1:T(8,128)(2,1)S(1)} %pad_maximum_fusion.2) | copy-start | bytes 491524
  258.3 5.1 %copy-start.9 = (bf16[128,2560]{1,0:T(8,128)(2,1)S(1)}, bf16[128,2560]{1,0:T(8,128)(2,1)}, u32[]{:S(2)}) copy-start(bf16[128,2560]{1,0:T(8,128)(2,1)} %copy-done.8) | copy-start | bytes 1966084
  266.6 3.7 copy-start.40
  266.6 106.5 %reduce-scatter.17.cloned.1.call-start = ((), (), s32[]{:S(2)}) async-start(), calls=%async_computation.15 | async-start | bytes 7864320 | tf_op jit(solution)/shard_map/reduce_scatter | solution.py:212
  266.6 4.6 %copy-start.11 = (bf16[128,2560]{1,0:T(8,128)(2,1)S(1)}, bf16[128,2560]{1,0:T(8,128)(2,1)}, u32[]{:S(2)}) copy-start(bf16[128,2560]{1,0:T(8,128)(2,1)} %copy-done.10) | copy-start | bytes 1966084
  276.1 179.6 %reduce-scatter.15.cloned.1.call-start = ((), (), s32[]{:S(2)}) async-start(), calls=%async_computation.14 | async-start | bytes 9830400 | tf_op jit(solution)/shard_map/reduce_scatter | solution.py:209
  288.0 16.9 %copy-start = (bf16[2,2,1,1,32,2560]{5,4,3,2,1,0:T(8,128)(2,1)S(1)}, bf16[2,2,1,1,32,2560]{5,4,3,2,1,0:T(8,128)(2,1)}, u32[]{:S(2)}) copy-start(bf16[2,2,1,1,32,2560]{5,4,3,2,1,0:T(8,128)(2,1)} %param.6) | copy-start | bytes 1966084
  288.0 16.9 %copy-start.48 = (f32[32]{0:T(128)S(1)}, f32[32]{0:T(128)}, u32[]{:S(2)}) copy-start(f32[32]{0:T(128)} %copy-done.47) | copy-start | bytes 388
  288.0 16.9 %copy-start.50 = (f32[32]{0:T(128)S(1)}, f32[32]{0:T(128)}, u32[]{:S(2)}) copy-start(f32[32]{0:T(128)} %copy-done.49) | copy-start | bytes 388
  288.0 54.4 %copy-start.13 = (bf16[32,2560]{1,0:T(8,128)(2,1)S(1)}, bf16[32,2560]{1,0:T(8,128)(2,1)}, u32[]{:S(2)}) copy-start(bf16[32,2560]{1,0:T(8,128)(2,1)} %copy-done.12) | copy-start | bytes 491524
  288.0 54.4 %copy-start.14 = (bf16[32,2560]{1,0:T(8,128)(2,1)S(1)}, bf16[32,2560]{1,0:T(8,128)(2,1)}, u32[]{:S(2)}) copy-start(bf16[32,2560]{1,0:T(8,128)(2,1)} %broadcast_select_fusion) | copy-start | bytes 491524
  (35 other events, 59.5 us)
Sparse Core Ops, SparseCore 0:
  104.7 24.0 reduce-scatter.8
  131.6 21.2 reduce-scatter.6
  258.1 23.2 reduce-scatter.12
  283.6 21.2 reduce-scatter.10
  307.6 65.4 reduce-scatter.16
  375.8 79.8 reduce-scatter.14
